TPU v7x, 32 devices: a whole 2x2x4 slice. The times are simulated.
32 devices in a mesh: row: 4 (over z), col: 8 (over y, x, core).
Axes of the slice: x: 2, y: 2, z: 4, core: 2. Of those that a mesh axis runs over, the one named last changes fastest.
Arguments:
- grad: float32 [8192, 14336], P(('row', 'col')), may hold values from -30 to 30
- momentum: float32 [8192, 14336], P(('row', 'col')), may hold values from -6 to 6
- weight: float32 [8192, 14336], P(('row', 'col')), may hold values from -0.75 to 0.75
Outputs:
- new_weight: float32 [8192, 14336], P('row', 'col')
- new_momentum: float32 [8192, 14336], P('row', 'col')
All inputs are finite; a program needn't handle non-finite values.
Results may differ from a plain program's by a relative error of at most 0.00002.
Values sent between devices are 32-bit elements; how exact they have to be, the bound alone decides.
A program may use at most 192 MiB of HBM per device.

v0:
```python
import math
import jax
import jax.numpy as jnp
from jax import lax
from jax.sharding import PartitionSpec as P

D = 8192
FF = 14336


def update_state(total, grad, momentum, weight):
    limit = jnp.float32(math.sqrt(D * FF))
    factor = jnp.minimum(jnp.float32(1.0), limit / (jnp.sqrt(total) + jnp.float32(1e-06)))
    new_momentum = jnp.float32(0.9) * momentum + factor * grad
    new_weight = weight - jnp.float32(0.1) * new_momentum
    return (new_weight, new_momentum)


def body(grad, momentum, weight):
    total = lax.psum(jnp.sum(grad * grad), ("row", "col"))
    local_weight, local_momentum = update_state(total, grad, momentum, weight)
    new_weight, new_momentum = (
        lax.all_to_all(local_weight, "col", split_axis=1, concat_axis=0, tiled=True),
        lax.all_to_all(local_momentum, "col", split_axis=1, concat_axis=0, tiled=True),
    )
    return (new_weight, new_momentum)


def solution(mesh):
    in_specs = (P(("row", "col"), None), P(("row", "col"), None), P(("row", "col"), None))
    out_specs = (P("row", "col"), P("row", "col"))
    return jax.shard_map(body, mesh=mesh, in_specs=in_specs, out_specs=out_specs, check_vma=False)
```

profile of v0, /device:TPU:0, one launch (start us, length us, event | category | flops | bytes accessed | tf_op | source)
XLA Modules:
  0.0 447.5 jit_solution(14981939035309159026)
XLA Ops:
  0.6 9.6 %multiply_reduce_fusion = f32[]{:T(128)} fusion(f32[256,14336]{1,0:T(8,128)} %param.3), kind=kLoop, calls=%fused_computation.4 | loop fusion | flops 7340031 | bytes 14680068 | tf_op jit(solution)/shard_map/reduce_sum | solution.py:20
  10.2 42.2 %psum.7 = f32[]{:T(128)} all-reduce(f32[]{:T(128)} %multiply_reduce_fusion), channel_id=1, replica_groups=mesh['row'=4,'col'=8] {'row','col'}, use_global_device_ids=true, to_apply=%region_1.0 | all-reduce | flops 1 | bytes 8 | tf_op jit(solution)/shard_map/psum | solution.py:20
  53.1 25.5 %multiply_subtract_fusion = (f32[256,14336]{1,0:T(8,128)}, f32[256,14336]{1,0:T(8,128)}) fusion(f32[256,14336]{1,0:T(8,128)} %param.5, f32[256,14336]{1,0:T(8,128)} %param.3, f32[]{:T(128)S(6)} %min_shard_map.3, f32[256,14336]{1,0:T(8,128)} %param.4), kind=kLoop, calls=%fused_computation.2 | loop fusion | flops 18350080 | bytes 73400320 | tf_op jit(solution)/shard_map/sub | solution.py:15
  78.6 11.8 %copy.11 = f32[32,8,8,1792]{3,2,0,1:T(8,128)} copy(f32[32,8,8,1792]{3,2,1,0:T(8,128)} %bitcast.17) | data formatting | bytes 29360128 | tf_op jit(solution)/shard_map/all_to_all | solution.py:24
  90.3 5.5 %all-to-all-start.1 = ((f32[256,8,1792]{2,0,1:T(8,128)}), f32[256,8,1792]{2,0,1:T(8,128)}, u32[]{:S(2)}, u32[]{:S(2)}) async-start(f32[256,8,1792]{2,0,1:T(8,128)} %bitcast.15), calls=%async_computation.1 | async-start | bytes 29360128 | tf_op jit(solution)/shard_map/all_to_all | solution.py:24
  95.9 12.0 %copy.12 = f32[32,8,8,1792]{3,2,0,1:T(8,128)} copy(f32[32,8,8,1792]{3,2,1,0:T(8,128)} %bitcast.16) | data formatting | bytes 29360128 | tf_op jit(solution)/shard_map/all_to_all | solution.py:23
  107.9 149.4 %all-to-all-done.1 = f32[256,8,1792]{2,0,1:T(8,128)} async-done(((f32[256,8,1792]{2,0,1:T(8,128)}), f32[256,8,1792]{2,0,1:T(8,128)}, u32[]{:S(2)}, u32[]{:S(2)}) %all-to-all-start.1) | async-done | bytes 14680096 | tf_op jit(solution)/shard_map/all_to_all | solution.py:24
  257.3 5.5 %all-to-all-start = ((f32[256,8,1792]{2,0,1:T(8,128)}), f32[256,8,1792]{2,0,1:T(8,128)}, u32[]{:S(2)}, u32[]{:S(2)}) async-start(f32[256,8,1792]{2,0,1:T(8,128)} %bitcast.14), calls=%async_computation | async-start | bytes 29360128 | tf_op jit(solution)/shard_map/all_to_all | solution.py:23
  262.9 161.5 %all-to-all-done = f32[256,8,1792]{2,0,1:T(8,128)} async-done(((f32[256,8,1792]{2,0,1:T(8,128)}), f32[256,8,1792]{2,0,1:T(8,128)}, u32[]{:S(2)}, u32[]{:S(2)}) %all-to-all-start) | async-done | bytes 14680096 | tf_op jit(solution)/shard_map/all_to_all | solution.py:23
  424.3 11.6 %copy.15 = f32[2048,1792]{1,0:T(8,128)} copy(f32[2048,1792]{1,0:T(8,128)} %bitcast.1) | data formatting | bytes 29360128
  435.9 11.6 %copy.16 = f32[2048,1792]{1,0:T(8,128)} copy(f32[2048,1792]{1,0:T(8,128)} %bitcast.3) | data formatting | bytes 29360128
Async XLA Ops:
  90.3 167.0 %all-to-all-start.1 = ((f32[256,8,1792]{2,0,1:T(8,128)}), f32[256,8,1792]{2,0,1:T(8,128)}, u32[]{:S(2)}, u32[]{:S(2)}) async-start(f32[256,8,1792]{2,0,1:T(8,128)} %bitcast.15), calls=%async_computation.1 | async-start | bytes 29360128 | tf_op jit(solution)/shard_map/all_to_all | solution.py:24
  257.3 167.0 %all-to-all-start = ((f32[256,8,1792]{2,0,1:T(8,128)}), f32[256,8,1792]{2,0,1:T(8,128)}, u32[]{:S(2)}, u32[]{:S(2)}) async-start(f32[256,8,1792]{2,0,1:T(8,128)} %bitcast.14), calls=%async_computation | async-start | bytes 29360128 | tf_op jit(solution)/shard_map/all_to_all | solution.py:23
where the time goes:
time: 448 us; the launch traced here: 447 us
  waiting for transfers between devices  311 us (69%)
  local copies, waits for them, and re-layouts  47 us (10%)
  blocking collectives  42.2 us (9%)
  other arithmetic  35 us (8%)
  starting transfers between devices  11.1 us (2%)
    all_to_all x1, waiting for transfers between devices, body(): lax.all_to_all(local_weight, 'col', split_axis=1, concat_axis=0, tiled=True)  161 us
    all_to_all x1, waiting for transfers between devices, body(): lax.all_to_all(local_momentum, 'col', split_axis=1, concat_axis=0, tiled=...  149 us
    psum x1, blocking collectives, body(): total = lax.psum(jnp.sum(grad * grad), ('row', 'col'))  42.2 us
    sub x1, other arithmetic, update_state(): new_weight = weight - jnp.float32(0.1) * new_momentum  25.5 us
    unnamed x2, local copies, waits for them, and re-layouts  23.2 us
    all_to_all x1, local copies, waits for them, and re-layouts, body(): lax.all_to_all(local_weight, 'col', split_axis=1, concat_axis=0, tiled=True)  12 us
    all_to_all x1, local copies, waits for them, and re-layouts, body(): lax.all_to_all(local_momentum, 'col', split_axis=1, concat_axis=0, tiled=...  11.8 us
    reduce_sum x1, other arithmetic, body(): total = lax.psum(jnp.sum(grad * grad), ('row', 'col'))  9.55 us
  transfers between devices with their start and end apart: 2, of which 2 were waited for; matrix products, arithmetic and copies ran while one was open for 3% of the time, Pallas kernels for 0%

commit v1 on v0

--- a/solution.py
+++ b/solution.py
@@ -21,7 +21,12 @@
     local_weight, local_momentum = update_state(total, grad, momentum, weight)
     new_weight, new_momentum = (
         lax.all_to_all(local_weight, "col", split_axis=1, concat_axis=0, tiled=True),
-        lax.all_to_all(local_momentum, "col", split_axis=1, concat_axis=0, tiled=True),
+        jnp.concatenate(
+            lax.all_to_all(
+                jnp.stack(jnp.split(local_momentum, lax.axis_size("col"), axis=1)), "col", 0, 0
+            ),
+            axis=0,
+        ),
     )
     return (new_weight, new_momentum)
 

time: 448 us -> 448 us (level)
  waiting for transfers between devices: 311 us -> 300 us
  local copies, waits for them, and re-layouts: 47 us -> 57.7 us
    all_to_all x1, waiting for transfers between devices: 161 us -> 139 us  [body(): lax.all_to_all(local_weight, 'col', split_axis=1, concat_axis=0, tiled=True)]
    unnamed x2 -> x9, local copies, waits for them, and re-layouts: 23.2 us -> 43.1 us
    all_to_all x1, waiting for transfers between devices: 149 us -> 161 us  [body(): lax.all_to_all(jnp.stack(jnp.split(local_momentum, lax.axis_size('col'),...]
    all_to_all x1 -> x0, local copies, waits for them, and re-layouts: 11.8 us -> none  [body(): lax.all_to_all(local_momentum, 'col', split_axis=1, concat_axis=0, tiled=...]
  transfers between devices with their start and end apart: 2 -> 2, of which waited for: 2 -> 2; matrix products, arithmetic and copies ran while one was open for 3% -> 5% of each run, Pallas kernels for 0% -> 0%
where the time goes in v1:
time: 448 us; the launch traced here: 447 us
  waiting for transfers between devices  300 us (67%)
  local copies, waits for them, and re-layouts  57.7 us (13%)
  blocking collectives  42.2 us (9%)
  other arithmetic  35 us (8%)
  starting transfers between devices  11.1 us (2%)
    all_to_all x1, waiting for transfers between devices, body(): lax.all_to_all(jnp.stack(jnp.split(local_momentum, lax.axis_size('col'),...  161 us
    all_to_all x1, waiting for transfers between devices, body(): lax.all_to_all(local_weight, 'col', split_axis=1, concat_axis=0, tiled=True)  139 us
    unnamed x9, local copies, waits for them, and re-layouts  43.1 us
    psum x1, blocking collectives, body(): total = lax.psum(jnp.sum(grad * grad), ('row', 'col'))  42.2 us
    sub x1, other arithmetic, update_state(): new_weight = weight - jnp.float32(0.1) * new_momentum  25.5 us
    all_to_all x1, local copies, waits for them, and re-layouts, body(): lax.all_to_all(local_weight, 'col', split_axis=1, concat_axis=0, tiled=True)  11.8 us
    reduce_sum x1, other arithmetic, body(): total = lax.psum(jnp.sum(grad * grad), ('row', 'col'))  9.55 us
  transfers between devices with their start and end apart: 2, of which 2 were waited for; matrix products, arithmetic and copies ran while one was open for 5% of the time, Pallas kernels for 0%

profile of v1, /device:TPU:0, one launch (start us, length us, event | category | flops | bytes accessed | tf_op | source)
XLA Modules:
  0.0 447.5 jit_solution(17594096824516680522)
XLA Ops:
  0.6 9.6 %multiply_reduce_fusion = f32[]{:T(128)} fusion(f32[256,14336]{1,0:T(8,128)} %param.3), kind=kLoop, calls=%fused_computation.3 | loop fusion | flops 7340031 | bytes 14680068 | tf_op jit(solution)/shard_map/reduce_sum | solution.py:20
  10.2 42.2 %psum.7 = f32[]{:T(128)} all-reduce(f32[]{:T(128)} %multiply_reduce_fusion), channel_id=1, replica_groups=mesh['row'=4,'col'=8] {'row','col'}, use_global_device_ids=true, to_apply=%region_1.0 | all-reduce | flops 1 | bytes 8 | tf_op jit(solution)/shard_map/psum | solution.py:20
  53.1 25.5 %multiply_subtract_fusion = (f32[256,14336]{1,0:T(8,128)}, f32[256,14336]{1,0:T(8,128)}) fusion(f32[256,14336]{1,0:T(8,128)} %param.5, f32[256,14336]{1,0:T(8,128)} %param.3, f32[]{:T(128)S(6)} %min_shard_map.3, f32[256,14336]{1,0:T(8,128)} %param.4), kind=kLoop, calls=%fused_computation.1 | loop fusion | flops 18350080 | bytes 73400320 | tf_op jit(solution)/shard_map/sub | solution.py:15
  78.6 11.8 %copy.8 = f32[32,8,8,1792]{3,2,0,1:T(8,128)} copy(f32[32,8,8,1792]{3,2,1,0:T(8,128)} %bitcast.41) | data formatting | bytes 29360128 | tf_op jit(solution)/shard_map/all_to_all | solution.py:23
  90.3 5.5 %all-to-all-start = ((f32[256,8,1792]{2,0,1:T(8,128)}), f32[256,8,1792]{2,0,1:T(8,128)}, u32[]{:S(2)}, u32[]{:S(2)}) async-start(f32[256,8,1792]{2,0,1:T(8,128)} %bitcast.40), calls=%async_computation | async-start | bytes 29360128 | tf_op jit(solution)/shard_map/all_to_all | solution.py:23
  95.9 2.8 fusion.7
  98.7 2.8 fusion.6
  101.6 2.8 fusion.5
  104.4 2.8 fusion.4
  107.3 2.8 fusion.3
  110.1 2.8 fusion.2
  112.9 2.8 fusion.1
  115.8 2.8 fusion
  118.6 138.7 %all-to-all-done = f32[256,8,1792]{2,0,1:T(8,128)} async-done(((f32[256,8,1792]{2,0,1:T(8,128)}), f32[256,8,1792]{2,0,1:T(8,128)}, u32[]{:S(2)}, u32[]{:S(2)}) %all-to-all-start) | async-done | bytes 14680096 | tf_op jit(solution)/shard_map/all_to_all | solution.py:23
  257.3 5.5 %all-to-all-start.1 = ((f32[8,256,1792]{2,1,0:T(8,128)}), f32[8,256,1792]{2,1,0:T(8,128)}, u32[]{:S(2)}, u32[]{:S(2)}) async-start(f32[8,256,1792]{2,1,0:T(8,128)} %fusion), calls=%async_computation.1 | async-start | bytes 29360128 | tf_op jit(solution)/shard_map/all_to_all | solution.py:25
  262.9 161.5 %all-to-all-done.1 = f32[8,256,1792]{2,1,0:T(8,128)} async-done(((f32[8,256,1792]{2,1,0:T(8,128)}), f32[8,256,1792]{2,1,0:T(8,128)}, u32[]{:S(2)}, u32[]{:S(2)}) %all-to-all-start.1) | async-done | bytes 14680096 | tf_op jit(solution)/shard_map/all_to_all | solution.py:25
  424.3 11.6 %copy.18 = f32[2048,1792]{1,0:T(8,128)} copy(f32[2048,1792]{1,0:T(8,128)} %bitcast.1) | data formatting | bytes 29360128
  435.9 11.6 %copy.19 = f32[2048,1792]{1,0:T(8,128)} copy(f32[2048,1792]{1,0:T(8,128)} %bitcast.10) | data formatting | bytes 29360128
Async XLA Ops:
  90.3 167.0 %all-to-all-start = ((f32[256,8,1792]{2,0,1:T(8,128)}), f32[256,8,1792]{2,0,1:T(8,128)}, u32[]{:S(2)}, u32[]{:S(2)}) async-start(f32[256,8,1792]{2,0,1:T(8,128)} %bitcast.40), calls=%async_computation | async-start | bytes 29360128 | tf_op jit(solution)/shard_map/all_to_all | solution.py:23
  257.3 167.0 %all-to-all-start.1 = ((f32[8,256,1792]{2,1,0:T(8,128)}), f32[8,256,1792]{2,1,0:T(8,128)}, u32[]{:S(2)}, u32[]{:S(2)}) async-start(f32[8,256,1792]{2,1,0:T(8,128)} %fusion), calls=%async_computation.1 | async-start | bytes 29360128 | tf_op jit(solution)/shard_map/all_to_all | solution.py:25
